TPU v7x, 32 devices: a whole 2x2x4 slice. The times are simulated.
32 devices in a mesh: row: 4 (over x, core), col: 8 (over z, y).
Axes of the slice: x: 2, y: 2, z: 4, core: 2. Of those that a mesh axis runs over, the one named last changes fastest.
Arguments:
- tail_vectors: float32 [16128, 4096], P('row', 'col'), may hold values from -6 to 6
- lower_panel: float32 [16128, 1024], P(('row', 'col')), may hold values from -0.046875 to 0.046875
- window_rhs: float32 [1024, 4096], P('row', 'col'), may hold values from -6 to 6
- window_block: float32 [1024, 1024], P(('row', 'col')), may hold values from -1 to 2, as said below
Outputs:
- window_vectors: float32 [1024, 4096], P('row', 'col')
Inputs may be any that keep to these rules, and one draw needn't show every extreme that they name: window_block is zero above the diagonal; its diagonal lies in 1 to 2; entries below the diagonal are under 1 / sqrt(1024) in magnitude.
All inputs are finite; a program needn't handle non-finite values.
Results may differ from a plain program's by a relative error of at most 0.000082.
Values sent between devices are 32-bit elements; how exact they have to be, the bound alone decides.
A program may use at most 128 MiB of HBM per device.

v0:
```python
import jax
import jax.numpy as jnp
from jax import lax
from jax.sharding import PartitionSpec as P


def per_device(tail_vectors, lower_panel, window_rhs, window_block):
    window = lower_panel.shape[1]
    block_full = lax.all_gather(window_block, ("row", "col"), axis=0, tiled=True)
    correction = lax.dot_general(
        lax.all_gather(lower_panel, "col", axis=0, tiled=True),
        tail_vectors,
        (((0,), (0,)), ((), ())),
        precision=lax.Precision.HIGHEST,
        preferred_element_type=jnp.float32,
    )
    row_share = window // lax.axis_size("row")
    offset = lax.axis_index("row") * row_share
    summand = -correction
    own_rows = lax.dynamic_slice_in_dim(summand, offset, row_share, 0) + window_rhs
    summand = lax.dynamic_update_slice_in_dim(summand, own_rows, offset, 0)
    column_part = lax.psum_scatter(summand, "row", scatter_dimension=1, tiled=True)
    solved = jax.scipy.linalg.solve_triangular(block_full, column_part, trans=1, lower=True)
    return lax.all_to_all(solved, "row", split_axis=0, concat_axis=1, tiled=True)


def solution(mesh):
    in_specs = (P("row", "col"), P(("row", "col"), None), P("row", "col"), P(("row", "col"), None))
    out_specs = P("row", "col")
    return jax.shard_map(
        per_device, mesh=mesh, in_specs=in_specs, out_specs=out_specs, check_vma=False
    )
```

profile of v0, /device:TPU:0, one launch (start us, length us, event | category | flops | bytes accessed | tf_op | source)
XLA Modules:
  0.0 439.2 jit_solution(12633628173417885095)
XLA Ops:
  6.5 0.7 all-gather.5.cloned.1.call-update
  7.3 0.7 all-gather.3.cloned.1.call-update
  8.1 228.3 %all-gather.5.cloned.1.call-done = f32[4032,1024]{1,0:T(8,128)} async-done(((f32[504,1024]{1,0:T(8,128)}), f32[4032,1024]{1,0:T(8,128)}) %all-gather.5.cloned.1.call-update) | async-done | bytes 16515088 | tf_op jit(solution)/shard_map/all_gather | solution.py:11
  236.3 30.2 %convolution_negate_fusion = f32[1024,512]{1,0:T(8,128)S(1)} fusion(f32[4032,1024]{1,0:T(8,128)} %all-gather.5.cloned.1.call-done, f32[4032,512]{1,0:T(8,128)} %param.4), kind=kOutput, calls=%fused_computation.4 | convolution fusion | flops 25367674880 | bytes 26869760 | tf_op jit(solution)/shard_map/dot_general | solution.py:10
  266.6 1.3 copy-done
  268.0 31.3 %all-gather.3.cloned.1.call-done = f32[1024,1024]{1,0:T(8,128)} async-done(((f32[32,1024]{1,0:T(8,128)}), f32[1024,1024]{1,0:T(8,128)}) %all-gather.3.cloned.1.call-update) | async-done | bytes 4194320 | tf_op jit(solution)/shard_map/all_gather | solution.py:9
  299.3 4.7 %fusion = f32[1024,1024]{1,0:T(8,128)} fusion(f32[1024,1024]{1,0:T(8,128)} %all-gather.3.cloned.1.call-done), kind=kLoop, calls=%fused_computation.3 | loop fusion | flops 2097152 | bytes 8388608 | tf_op jit(solution)/shard_map/jit(_solve_triangular)/triangular_solve | solution.py:23
  304.1 23.9 %while.1 = (s32[]{:T(128)}, f32[1024,1024]{1,0:T(8,128)}, s32[8,2]{0,1:T(2,128)S(1)}, f32[8,128,128]{2,1,0:T(8,128)S(1)}, s32[]{:T(128)}) while((s32[]{:T(128)}, f32[1024,1024]{1,0:T(8,128)}, s32[8,2]{0,1:T(2,128)S(1)}, f32[8,128,128]{2,1,0:T(8,128)S(1)}, s32[]{:T(128)}) %tuple.22), condition=%wide.while_cond, body=%wide.while_body.sunk | while | flops 2 | bytes 131189 | solution.py:23
  304.7 2.3 bitcast_dynamic-update-slice_fusion.2
  307.1 0.6 fusion.50
  307.7 2.3 bitcast_dynamic-update-slice_fusion.2
  310.2 0.6 fusion.50
  310.7 2.3 bitcast_dynamic-update-slice_fusion.2
  313.1 0.6 fusion.50
  313.7 2.3 bitcast_dynamic-update-slice_fusion.2
  316.1 0.6 fusion.50
  316.7 2.3 bitcast_dynamic-update-slice_fusion.2
  319.1 0.6 fusion.50
  319.7 2.3 bitcast_dynamic-update-slice_fusion.2
  322.7 2.3 bitcast_dynamic-update-slice_fusion.2
  325.7 2.2 bitcast_dynamic-update-slice_fusion.2
  328.0 78.8 %custom-call.4 = f32[8,128,128]{1,2,0:T(8,128)S(1)} custom-call(f32[8,128,128]{2,1,0:T(8,128)S(1)} %get-tuple-element.12), custom_call_target="InvertDiagBlocksLowerTriangular" | custom-call | tf_op jit(solution)/shard_map/jit(_solve_triangular)/triangular_solve | solution.py:23
  406.8 1.0 fusion.22
  407.8 1.2 convolution_subtract_fusion.4
  409.2 1.3 convolution_subtract_fusion.3
  410.7 1.4 convolution_subtract_fusion.6
  412.4 1.6 convolution_subtract_fusion.5
  414.2 1.7 convolution_subtract_fusion.2
  416.2 1.8 convolution_subtract_fusion.1
  418.3 1.9 convolution_subtract_fusion
  420.6 11.2 %all_to_all.19 = f32[4,256,128]{2,1,0:T(8,128)S(1)} all-to-all(f32[4,256,128]{2,1,0:T(8,128)S(1)} %bitcast.60), channel_id=1, replica_groups=mesh['row'=4,'col'=8] {'row'}, dimensions={0} | all-to-all | bytes 1048576 | tf_op jit(solution)/shard_map/all_to_all | solution.py:24
  431.8 0.9 copy_bitcast_fusion
  (52 shorter events, 4.2 us)
Async XLA Ops:
  6.5 229.8 %all-gather.5.cloned.1.call-start = ((), (), s32[]{:S(2)}) async-start(), calls=%async_computation.3 | async-start | bytes 18579456 | tf_op jit(solution)/shard_map/all_gather | solution.py:11
  7.3 292.1 %all-gather.3.cloned.1.call-start = ((), (), s32[]{:S(2)}) async-start(), calls=%async_computation.2 | async-start | bytes 4325376 | tf_op jit(solution)/shard_map/all_gather | solution.py:9
  8.0 398.8 %reduce-scatter.2.cloned.1.call-start = ((), (), s32[]{:S(2)}) async-start(), calls=%async_computation.4 | async-start | bytes 2621440 | tf_op jit(solution)/shard_map/reduce_scatter | solution.py:22
  8.1 258.4 %copy-start.1 = (f32[256,512]{1,0:T(8,128)S(1)}, f32[256,512]{1,0:T(8,128)}, u32[]{:S(2)}) copy-start(f32[256,512]{1,0:T(8,128)} %param.6) | copy-start | bytes 1572868
  266.6 1.3 copy-start
Sparse Core Ops, SparseCore 0:
  9.5 226.7 all-gather.4
  239.4 59.8 all-gather.2
  301.9 29.9 reduce-scatter.1
where the time goes:
time: 440 us; the launch traced here: 439 us
  waiting for transfers between devices  261 us (59%)
  other arithmetic  83.6 us (19%)
  matrix products  43.5 us (10%)
  local copies, waits for them, and re-layouts  26.1 us (6%)
  between operations  13.5 us (3%)
  blocking collectives  11.2 us (3%)
    all_gather x1, waiting for transfers between devices, per_device(): lax.all_gather(lower_panel, 'col', axis=0, tiled=True)  228 us
    another operation x3, other arithmetic, per_device(): jax.scipy.linalg.solve_triangular(block_full, column_part, trans=1, lower...  83.5 us
    all_gather x1, waiting for transfers between devices, per_device(): lax.all_gather(window_block, ('row', 'col'), axis=0, tiled=True)  31.3 us
    dot_general x1, matrix products, per_device(): lax.dot_general(lax.all_gather(lower_panel, 'col', axis=0, tiled=True), t...  30.2 us
    another operation x24, local copies, waits for them, and re-layouts  23.8 us
    another operation x15, matrix products, per_device(): jax.scipy.linalg.solve_triangular(block_full, column_part, trans=1, lower...  13.3 us
    all_to_all x1, blocking collectives, per_device(): lax.all_to_all(solved, 'row', split_axis=0, concat_axis=1, tiled=True)  11.2 us
  transfers between devices with their start and end apart: 3, of which 2 were waited for; matrix products, arithmetic and copies ran while one was open for 31% of the time, Pallas kernels for 0%

commit v1 on v0

v1 whole, which is shorter than its diff:
```python
import functools

import jax
import jax.numpy as jnp
from jax import lax
from jax.experimental import pallas as pl
from jax.experimental.pallas import tpu as pltpu
from jax.sharding import PartitionSpec as P

MESH = pl.DeviceIdType.MESH
HIGHEST = lax.Precision.HIGHEST


def ring_sides(n):
    y = 1
    while (2 * y) * (2 * y) <= n:
        y *= 2
    return n // y, y


def col_of_position(pos, n):
    zs, ys = ring_sides(n)
    rest = jnp.maximum(pos - zs, 0)
    row = rest // (ys - 1)
    within = rest % (ys - 1)
    y = jnp.where(row % 2 == 0, 1 + within, ys - 1 - within)
    return jnp.where(pos < zs, pos * ys, (zs - 1 - row) * ys + y)


def position_of_col(col, n):
    zs, ys = ring_sides(n)
    z, y = col // ys, col % ys
    row = zs - 1 - z
    within = jnp.where(row % 2 == 0, y - 1, ys - 1 - y)
    return jnp.where(y == 0, z, zs + row * (ys - 1) + within)


def dot(a, b):
    return jnp.dot(a, b, precision=HIGHEST, preferred_element_type=jnp.float32)


def dot_t(a, b):
    return lax.dot_general(
        a, b, (((0,), (0,)), ((), ())), precision=HIGHEST, preferred_element_type=jnp.float32
    )


def lower_inverse(block, base=32):
    size = block.shape[0]
    rows = lax.broadcasted_iota(jnp.int32, (size, size), 0)
    cols = lax.broadcasted_iota(jnp.int32, (size, size), 1)
    eye = jnp.where(rows == cols, 1.0, 0.0)
    diag_col = jnp.sum(jnp.where(rows == cols, block, 0.0), axis=1, keepdims=True)
    diag_row = jnp.sum(jnp.where(rows == cols, block, 0.0), axis=0, keepdims=True)
    near = (rows // base == cols // base) & (rows > cols)
    power = jnp.where(near, -block / diag_col, 0.0)
    inverse = eye + power
    reach = 2
    while reach < base:
        power = dot(power, power)
        inverse = inverse + dot(inverse, power)
        reach *= 2
    inverse = inverse / diag_row
    while base < size:
        below = (rows // (2 * base) == cols // (2 * base)) & (rows // base > cols // base)
        inverse = inverse - dot(dot(inverse, jnp.where(below, block, 0.0)), inverse)
        base *= 2
    return inverse


def kernel(
    n, groups, tail_hbm, panel_hbm, block_hbm, rhs_ref, out_ref,
    tail, buf, acc, strip, inverse, solved, parts, landed,
    tail_sem, load_sem, send_sem, recv_sem, part_send, part_recv,
):
    half = n // 2
    depth = panel_hbm.shape[0]
    thin = block_hbm.shape[0]
    width = buf.shape[-1]
    r = lax.axis_index("row")
    me = position_of_col(lax.axis_index("col"), n)
    right = col_of_position((me + 1) % n, n)
    left = col_of_position((me + n - 1) % n, n)

    tail_copy = pltpu.make_async_copy(tail_hbm, tail, tail_sem)

    def loads(g):
        cols = pl.ds(pl.multiple_of((groups - 1 - g) * width, width), width)
        return (
            pltpu.make_async_copy(panel_hbm.at[:, cols], buf.at[0, g, pl.ds(0, depth)], load_sem.at[0, g]),
            pltpu.make_async_copy(block_hbm.at[:, cols], buf.at[0, g, pl.ds(depth, thin)], load_sem.at[1, g]),
        )

    def start_loads(g, _):
        for copy in loads(g):
            copy.start()
        return 0

    lax.fori_loop(0, groups, start_loads, 0)
    tail_copy.start()

    barrier = pltpu.get_barrier_semaphore()
    for side in (left, right):
        pl.semaphore_signal(barrier, inc=1, device_id={"col": side}, device_id_type=MESH)
    for k in range(1, groups):
        pl.semaphore_signal(barrier, inc=1, device_id={"row": (r + k) % groups}, device_id_type=MESH)
    pl.semaphore_wait(barrier, 2 + groups - 1)

    def hop(way, g, d):
        source = d - 1 if way == 0 else (n - (d - 1)) % n
        target = d if way == 0 else n - d
        return pltpu.make_async_remote_copy(
            src_ref=buf.at[source, g],
            dst_ref=buf.at[target, g],
            send_sem=send_sem.at[way, g, d - 1],
            recv_sem=recv_sem.at[way, g, d - 1],
            device_id={"col": right if way == 0 else left},
            device_id_type=MESH,
        )

    def send_own(g):
        for copy in loads(g):
            copy.wait()
        for way in range(2):
            hop(way, g, 1).start()

    def use(slot, g):
        origin = col_of_position((me + n - slot) % n, n)
        rows = pl.ds(pl.multiple_of(origin * depth, 8), depth)
        acc[...] += dot_t(buf[slot, g, pl.ds(0, depth)], tail[rows, :])
        strip[pl.ds(pl.multiple_of(origin * thin, 8), thin), :] = buf[slot, g, pl.ds(depth, thin)]

    def part_copy(q):
        return pltpu.make_async_remote_copy(
            src_ref=parts.at[q],
            dst_ref=landed.at[r],
            send_sem=part_send.at[q],
            recv_sem=part_recv.at[r],
            device_id={"row": q},
            device_id_type=MESH,
        )

    def finish(q):
        total = parts[q]
        for k in range(1, groups):
            other = (r + k) % groups
            pltpu.make_async_remote_copy(
                src_ref=parts.at[q],
                dst_ref=landed.at[other],
                send_sem=part_send.at[q],
                recv_sem=part_recv.at[other],
                device_id={"row": other},
                device_id_type=MESH,
            ).wait_recv()
            total = total + landed[other]
        solved[...] = dot_t(inverse[...], total)
        out_ref[...] = solved[...]

    send_own(0)
    tail_copy.wait()

    def group(g, _):
        q = groups - 1 - g

        @pl.when(g + 1 < groups)
        def _():
            send_own(g + 1)

        acc[...] = jnp.zeros_like(acc)
        use(0, g)

        def step(d, _):
            for way in range(2):
                hop(way, g, d).wait_recv()
                onward = d + 1 < half
                last = (d + 1 == half) & (g % 2 == way)

                @pl.when(onward | last)
                def _():
                    hop(way, g, d + 1).start()

            def both(way, _):
                use(jnp.where(way == 0, d, n - d), g)
                return 0

            lax.fori_loop(0, 2, both, 0)

            @pl.when((d == half - 1) & (r == q + 1))
            def _():
                finish(q + 1)

            return 0

        lax.fori_loop(1, half, step, 0)
        for way in range(2):
            @pl.when(g % 2 == way)
            def _():
                hop(way, g, half).wait_recv()

        use(half, g)

        parts[q] = -acc[...]

        @pl.when(r == q)
        def _():
            parts[q] += rhs_ref[...]

        @pl.when(r > q)
        def _():
            parts[q] -= dot_t(strip[...], solved[...])

        @pl.when(r != q)
        def _():
            part_copy(q).start()

        @pl.when(r == q)
        def _():
            inverse[...] = lower_inverse(strip[...])

        return 0

    lax.fori_loop(0, groups, group, 0)

    @pl.when(r == 0)
    def _():
        finish(0)

    def drain(g, _):
        def one(d, _):
            for way in range(2):
                @pl.when((d < half) | (g % 2 == way))
                def _():
                    hop(way, g, d).wait_send()
            return 0

        lax.fori_loop(1, half + 1, one, 0)

        @pl.when(r != g)
        def _():
            part_copy(g).wait_send()

        return 0

    lax.fori_loop(0, groups, drain, 0)


def per_device(n, groups, tail_vectors, lower_panel, window_rhs, window_block):
    tail_rows, columns = tail_vectors.shape
    depth, window = lower_panel.shape
    thin = window_block.shape[0]
    width = window // groups
    half = n // 2
    f32 = jnp.float32
    anywhere = pl.BlockSpec(memory_space=pl.ANY)
    vmem = pl.BlockSpec(memory_space=pltpu.VMEM)
    return pl.pallas_call(
        functools.partial(kernel, n, groups),
        out_shape=jax.ShapeDtypeStruct((width, columns), f32),
        in_specs=[anywhere, anywhere, anywhere, vmem],
        out_specs=vmem,
        scratch_shapes=[
            pltpu.VMEM((tail_rows, columns), f32),
            pltpu.VMEM((n, groups, depth + thin, width), f32),
            pltpu.VMEM((width, columns), f32),
            pltpu.VMEM((width, width), f32),
            pltpu.VMEM((width, width), f32),
            pltpu.VMEM((width, columns), f32),
            pltpu.VMEM((groups, width, columns), f32),
            pltpu.VMEM((groups, width, columns), f32),
            pltpu.SemaphoreType.DMA,
            pltpu.SemaphoreType.DMA((2, groups)),
            pltpu.SemaphoreType.DMA((2, groups, half)),
            pltpu.SemaphoreType.DMA((2, groups, half)),
            pltpu.SemaphoreType.DMA((groups,)),
            pltpu.SemaphoreType.DMA((groups,)),
        ],
        compiler_params=pltpu.CompilerParams(
            collective_id=0, has_side_effects=True, vmem_limit_bytes=60 * 1024 * 1024
        ),
    )(tail_vectors, lower_panel, window_block, window_rhs)


def solution(mesh):
    in_specs = (P("row", "col"), P(("row", "col"), None), P("row", "col"), P(("row", "col"), None))
    out_specs = P("row", "col")
    body = functools.partial(per_device, mesh.shape["col"], mesh.shape["row"])
    return jax.shard_map(body, mesh=mesh, in_specs=in_specs, out_specs=out_specs, check_vma=False)
```

time: 440 us -> 223 us (0.51)
  waiting for transfers between devices: 261 us -> 0 us
  Pallas kernels: 0 us -> 221 us
  other arithmetic: 83.6 us -> 0 us
  matrix products: 43.5 us -> 0 us
  local copies, waits for them, and re-layouts: 26.1 us -> 1.87 us
  between operations: 13.5 us -> 0.01 us
  blocking collectives: 11.2 us -> 0 us
    all_gather x2 -> x0, waiting for transfers between devices: 260 us -> none  [the longest x1 228 us: per_device(): lax.all_gather(lower_panel, 'col', axis=0, tiled=True)]
    pallas_call x0 -> x1, Pallas kernels: none -> 221 us  [per_device(): pl.pallas_call(functools.partial(kernel, n, groups), out_shape=jax.ShapeD...]
    another operation x3 -> x0, other arithmetic: 83.5 us -> none  [per_device(): jax.scipy.linalg.solve_triangular(block_full, column_part, trans=1, lower...]
    dot_general x1 -> x0, matrix products: 30.2 us -> none  [per_device(): lax.dot_general(lax.all_gather(lower_panel, 'col', axis=0, tiled=True), t...]
    another operation x29 -> x0, local copies, waits for them, and re-layouts: 23.8 us -> none
    another operation x15 -> x0, matrix products: 13.3 us -> none  [per_device(): jax.scipy.linalg.solve_triangular(block_full, column_part, trans=1, lower...]
    all_to_all x1 -> x0, blocking collectives: 11.2 us -> none  [per_device(): lax.all_to_all(solved, 'row', split_axis=0, concat_axis=1, tiled=True)]
  transfers between devices with their start and end apart: 3 -> 0, of which waited for: 2 -> 0; matrix products, arithmetic and copies ran while one was open for 31% -> 0% of each run, Pallas kernels for 0% -> 0%
where the time goes in v1:
time: 223 us
  Pallas kernels  221 us (99%)
    pallas_call x1, Pallas kernels, per_device(): pl.pallas_call(functools.partial(kernel, n, groups), out_shape=jax.ShapeD...  221 us

profile of v1, /device:TPU:0, one launch (start us, length us, event | category | flops | bytes accessed | tf_op | source)
XLA Modules:
  0.0 222.8 jit_solution(17634675319693908912)
XLA Ops:
  0.0 220.9 %shard_map.46 = f32[256,512]{1,0:T(8,128)} custom-call(f32[4032,512]{1,0:T(8,128)} %tail_hbm.1, f32[504,1024]{1,0:T(8,128)} %panel_hbm.1, f32[32,1024]{1,0:T(8,128)} %block_hbm.1, f32[256,512]{1,0:T(8,128)} %rhs_ref.1), custom_call_target="tpu_custom_call" | custom-call | tf_op jit(solution)/shard_map/pallas_call | solution.py:256
  220.9 1.9 copy.6

commit v2 on v1

v2 whole, which is shorter than its diff:
```python
import functools

import jax
import jax.numpy as jnp
from jax import lax
from jax.experimental import pallas as pl
from jax.experimental.pallas import tpu as pltpu
from jax.sharding import PartitionSpec as P

MESH = pl.DeviceIdType.MESH
HIGHEST = lax.Precision.HIGHEST


def ring_sides(n):
    y = 1
    while (2 * y) * (2 * y) <= n:
        y *= 2
    return n // y, y


def col_of_position(pos, n):
    zs, ys = ring_sides(n)
    rest = jnp.maximum(pos - zs, 0)
    row = rest // (ys - 1)
    within = rest % (ys - 1)
    y = jnp.where(row % 2 == 0, 1 + within, ys - 1 - within)
    return jnp.where(pos < zs, pos * ys, (zs - 1 - row) * ys + y)


def position_of_col(col, n):
    zs, ys = ring_sides(n)
    z, y = col // ys, col % ys
    row = zs - 1 - z
    within = jnp.where(row % 2 == 0, y - 1, ys - 1 - y)
    return jnp.where(y == 0, z, zs + row * (ys - 1) + within)


def dot(a, b):
    return jnp.dot(a, b, precision=HIGHEST, preferred_element_type=jnp.float32)


def dot_t(a, b):
    return lax.dot_general(
        a, b, (((0,), (0,)), ((), ())), precision=HIGHEST, preferred_element_type=jnp.float32
    )


def lower_inverse(block, base=32):
    size = block.shape[0]
    rows = lax.broadcasted_iota(jnp.int32, (size, size), 0)
    cols = lax.broadcasted_iota(jnp.int32, (size, size), 1)
    eye = jnp.where(rows == cols, 1.0, 0.0)
    diag_col = jnp.sum(jnp.where(rows == cols, block, 0.0), axis=1, keepdims=True)
    diag_row = jnp.sum(jnp.where(rows == cols, block, 0.0), axis=0, keepdims=True)
    near = (rows // base == cols // base) & (rows > cols)
    power = jnp.where(near, -block / diag_col, 0.0)
    inverse = eye + power
    reach = 2
    while reach < base:
        power = dot(power, power)
        inverse = inverse + dot(inverse, power)
        reach *= 2
    inverse = inverse / diag_row
    while base < size:
        below = (rows // (2 * base) == cols // (2 * base)) & (rows // base > cols // base)
        inverse = inverse - dot(dot(inverse, jnp.where(below, block, 0.0)), inverse)
        base *= 2
    return inverse


WIDTH = 128
STRIDE_D, STRIDE_G = 4, 3


def kernel(
    n, rows_axis, tail_hbm, panel_hbm, block_hbm, rhs_ref, out_ref,
    tail, buf, strips, inverse, solved, parts, landed,
    tail_sem, load_sem, send_sem, recv_sem, part_send, part_recv,
):
    half = n // 2
    depth = panel_hbm.shape[0]
    thin = block_hbm.shape[0]
    groups, width = buf.shape[1], buf.shape[-1]
    per_row = groups // rows_axis
    r = lax.axis_index("row")
    me = position_of_col(lax.axis_index("col"), n)
    right = col_of_position((me + 1) % n, n)
    left = col_of_position((me + n - 1) % n, n)

    def loads(g):
        cols = pl.ds(pl.multiple_of((groups - 1 - g) * width, width), width)
        return (
            pltpu.make_async_copy(panel_hbm.at[:, cols], buf.at[0, g, pl.ds(0, depth)], load_sem.at[0, g]),
            pltpu.make_async_copy(block_hbm.at[:, cols], buf.at[0, g, pl.ds(depth, thin)], load_sem.at[1, g]),
        )

    def start_loads(g, _):
        for copy in loads(g):
            copy.start()
        return 0

    lax.fori_loop(0, groups, start_loads, 0)
    tail_copy = pltpu.make_async_copy(tail_hbm, tail, tail_sem)
    tail_copy.start()

    barrier = pltpu.get_barrier_semaphore()
    for side in (left, right):
        pl.semaphore_signal(barrier, inc=1, device_id={"col": side}, device_id_type=MESH)
    for k in range(1, rows_axis):
        pl.semaphore_signal(barrier, inc=1, device_id={"row": (r + k) % rows_axis}, device_id_type=MESH)
    pl.semaphore_wait(barrier, 2 + rows_axis - 1)

    def hop(way, g, d):
        source = d - 1 if way == 0 else (n - (d - 1)) % n
        target = d if way == 0 else n - d
        return pltpu.make_async_remote_copy(
            src_ref=buf.at[source, g],
            dst_ref=buf.at[target, g],
            send_sem=send_sem.at[way, g, d - 1],
            recv_sem=recv_sem.at[way, g, d - 1],
            device_id={"col": right if way == 0 else left},
            device_id_type=MESH,
        )

    def use(slot, g):
        origin = col_of_position((me + n - slot) % n, n)
        rows = pl.ds(pl.multiple_of(origin * depth, 8), depth)
        parts[g] -= dot_t(buf[slot, g, pl.ds(0, depth)], tail[rows, :])
        strips[g, pl.ds(pl.multiple_of(origin * thin, 8), thin), :] = buf[slot, g, pl.ds(depth, thin)]

    def part_copy(g, source, owner):
        slot = (groups - 1 - g) % per_row
        return pltpu.make_async_remote_copy(
            src_ref=parts.at[g],
            dst_ref=landed.at[slot, source],
            send_sem=part_send.at[g],
            recv_sem=part_recv.at[slot, source],
            device_id={"row": owner},
            device_id_type=MESH,
        )

    def place(g):
        return pl.ds(pl.multiple_of(((groups - 1 - g) % per_row) * width, width), width)

    def owner_of(g):
        return (groups - 1 - g) // per_row

    def finish(g):
        total = parts[g]
        for k in range(1, rows_axis):
            other = (r + k) % rows_axis
            part_copy(g, other, other).wait_recv()
            total = total + landed[(groups - 1 - g) % per_row, other]
        result = dot_t(inverse[...], total)
        solved[place(g), :] = result
        out_ref[place(g), :] = result

    def clear(g, _):
        parts[g] = jnp.zeros_like(parts[g])

        @pl.when(r == owner_of(g))
        def _():
            parts[g] = rhs_ref[place(g), :]

        return 0

    lax.fori_loop(0, groups, clear, 0)
    solved[...] = jnp.zeros_like(solved)

    def complete(g):
        @pl.when((g > 0) & (r == owner_of(g - 1)))
        def _():
            finish(g - 1)

        @pl.when(r >= owner_of(g))
        def _():
            parts[g] -= dot_t(strips[g], solved[...])

        @pl.when(r != owner_of(g))
        def _():
            part_copy(g, r, owner_of(g)).start()

        @pl.when(r == owner_of(g))
        def _():
            inverse[...] = lower_inverse(strips[g, place(g), :])

    def item(g, d):
        @pl.when(d == 0)
        def _():
            for copy in loads(g):
                copy.wait()
            for way in range(2):
                hop(way, g, 1).start()

        @pl.when((d == 0) & (g == 0))
        def _():
            tail_copy.wait()

        for way in range(2):
            @pl.when((d > 0) & ((d < half) | (g % 2 == way)))
            def _():
                hop(way, g, d).wait_recv()

            @pl.when((d > 0) & ((d + 1 < half) | ((d + 1 == half) & (g % 2 == way))))
            def _():
                hop(way, g, d + 1).start()

        def one(way, _):
            use(jnp.where(way == 0, d, n - d), g)
            return 0

        lax.fori_loop(0, jnp.where((d == 0) | (d == half), 1, 2), one, 0)

        @pl.when(d == half)
        def _():
            complete(g)

    def diagonal(k, _):
        def one(g, _):
            rest = k - STRIDE_G * g

            @pl.when((rest >= 0) & (rest <= STRIDE_D * half) & (rest % STRIDE_D == 0))
            def _():
                item(g, rest // STRIDE_D)

            return 0

        lax.fori_loop(0, groups, one, 0)
        return 0

    lax.fori_loop(0, STRIDE_D * half + STRIDE_G * (groups - 1) + 1, diagonal, 0)

    @pl.when(r == 0)
    def _():
        finish(groups - 1)

    def drain(g, _):
        def one(d, _):
            for way in range(2):
                @pl.when((d < half) | (g % 2 == way))
                def _():
                    hop(way, g, d).wait_send()
            return 0

        lax.fori_loop(1, half + 1, one, 0)

        @pl.when(r != owner_of(g))
        def _():
            part_copy(g, r, owner_of(g)).wait_send()

        return 0

    lax.fori_loop(0, groups, drain, 0)


def per_device(n, rows_axis, tail_vectors, lower_panel, window_rhs, window_block):
    tail_rows, columns = tail_vectors.shape
    depth, window = lower_panel.shape
    thin = window_block.shape[0]
    share = window // rows_axis
    width = min(WIDTH, share)
    groups = window // width
    half = n // 2
    f32 = jnp.float32
    anywhere = pl.BlockSpec(memory_space=pl.ANY)
    vmem = pl.BlockSpec(memory_space=pltpu.VMEM)
    return pl.pallas_call(
        functools.partial(kernel, n, rows_axis),
        out_shape=jax.ShapeDtypeStruct((share, columns), f32),
        in_specs=[anywhere, anywhere, anywhere, vmem],
        out_specs=vmem,
        scratch_shapes=[
            pltpu.VMEM((tail_rows, columns), f32),
            pltpu.VMEM((n, groups, depth + thin, width), f32),
            pltpu.VMEM((groups, share, width), f32),
            pltpu.VMEM((width, width), f32),
            pltpu.VMEM((share, columns), f32),
            pltpu.VMEM((groups, width, columns), f32),
            pltpu.VMEM((share // width, rows_axis, width, columns), f32),
            pltpu.SemaphoreType.DMA,
            pltpu.SemaphoreType.DMA((2, groups)),
            pltpu.SemaphoreType.DMA((2, groups, half)),
            pltpu.SemaphoreType.DMA((2, groups, half)),
            pltpu.SemaphoreType.DMA((groups,)),
            pltpu.SemaphoreType.DMA((share // width, rows_axis)),
        ],
        compiler_params=pltpu.CompilerParams(
            collective_id=0, has_side_effects=True, vmem_limit_bytes=60 * 1024 * 1024
        ),
    )(tail_vectors, lower_panel, window_block, window_rhs)


def solution(mesh):
    in_specs = (P("row", "col"), P(("row", "col"), None), P("row", "col"), P(("row", "col"), None))
    out_specs = P("row", "col")
    body = functools.partial(per_device, mesh.shape["col"], mesh.shape["row"])
    return jax.shard_map(body, mesh=mesh, in_specs=in_specs, out_specs=out_specs, check_vma=False)
```

time: 223 us -> 190 us (0.85)
  Pallas kernels: 221 us -> 188 us
    pallas_call x1, Pallas kernels: 221 us -> 188 us  [per_device(): pl.pallas_call(functools.partial(kernel, n, rows_axis), out_shape=jax.Sha...]
where the time goes in v2:
time: 190 us
  Pallas kernels  188 us (99%)
    pallas_call x1, Pallas kernels, per_device(): pl.pallas_call(functools.partial(kernel, n, rows_axis), out_shape=jax.Sha...  188 us

profile of v2, /device:TPU:0, one launch (start us, length us, event | category | flops | bytes accessed | tf_op | source)
XLA Modules:
  0.0 189.7 jit_solution(18074764060728184662)
XLA Ops:
  0.0 187.8 %shard_map.46 = f32[256,512]{1,0:T(8,128)} custom-call(f32[4032,512]{1,0:T(8,128)} %tail_hbm.1, f32[504,1024]{1,0:T(8,128)} %panel_hbm.1, f32[32,1024]{1,0:T(8,128)} %block_hbm.1, f32[256,512]{1,0:T(8,128)} %rhs_ref.1), custom_call_target="tpu_custom_call" | custom-call | tf_op jit(solution)/shard_map/pallas_call | solution.py:267
  187.8 1.9 copy.6

commit v3 on v2

--- a/solution.py
+++ b/solution.py
@@ -73,9 +73,9 @@
 
 
 def kernel(
-    n, rows_axis, tail_hbm, panel_hbm, block_hbm, rhs_ref, out_ref,
-    tail, buf, strips, inverse, solved, parts, landed,
-    tail_sem, load_sem, send_sem, recv_sem, part_send, part_recv,
+    n, rows_axis, tail_hbm, panel_hbm, block_hbm, rhs_hbm, out_ref,
+    tail, rhs, buf, strips, inverse, solved, parts, landed,
+    tail_sem, rhs_sem, load_sem, send_sem, recv_sem, part_send, part_recv,
 ):
     half = n // 2
     depth = panel_hbm.shape[0]
@@ -101,6 +101,8 @@
 
     lax.fori_loop(0, groups, start_loads, 0)
     tail_copy = pltpu.make_async_copy(tail_hbm, tail, tail_sem)
+    rhs_copy = pltpu.make_async_copy(rhs_hbm, rhs, rhs_sem)
+    rhs_copy.start()
     tail_copy.start()
 
     barrier = pltpu.get_barrier_semaphore()
@@ -160,12 +162,9 @@
 
         @pl.when(r == owner_of(g))
         def _():
-            parts[g] = rhs_ref[place(g), :]
+            parts[g] = rhs[place(g), :]
 
         return 0
-
-    lax.fori_loop(0, groups, clear, 0)
-    solved[...] = jnp.zeros_like(solved)
 
     def complete(g):
         @pl.when((g > 0) & (r == owner_of(g - 1)))
@@ -194,6 +193,9 @@
 
         @pl.when((d == 0) & (g == 0))
         def _():
+            rhs_copy.wait()
+            lax.fori_loop(0, groups, clear, 0)
+            solved[...] = jnp.zeros_like(solved)
             tail_copy.wait()
 
         for way in range(2):
@@ -267,16 +269,18 @@
     return pl.pallas_call(
         functools.partial(kernel, n, rows_axis),
         out_shape=jax.ShapeDtypeStruct((share, columns), f32),
-        in_specs=[anywhere, anywhere, anywhere, vmem],
+        in_specs=[anywhere] * 4,
         out_specs=vmem,
         scratch_shapes=[
             pltpu.VMEM((tail_rows, columns), f32),
+            pltpu.VMEM((share, columns), f32),
             pltpu.VMEM((n, groups, depth + thin, width), f32),
             pltpu.VMEM((groups, share, width), f32),
             pltpu.VMEM((width, width), f32),
             pltpu.VMEM((share, columns), f32),
             pltpu.VMEM((groups, width, columns), f32),
             pltpu.VMEM((share // width, rows_axis, width, columns), f32),
+            pltpu.SemaphoreType.DMA,
             pltpu.SemaphoreType.DMA,
             pltpu.SemaphoreType.DMA((2, groups)),
             pltpu.SemaphoreType.DMA((2, groups, half)),

time: 190 us -> 189 us (level)
  no operation moved by 1% of the time
where the time goes in v3:
time: 189 us; the launch traced here: 188 us
  Pallas kernels  187 us (99%)
    pallas_call x1, Pallas kernels, per_device(): pl.pallas_call(functools.partial(kernel, n, rows_axis), out_shape=jax.Sha...  187 us

profile of v3, /device:TPU:0, one launch (start us, length us, event | category | flops | bytes accessed | tf_op | source)
XLA Modules:
  0.0 188.4 jit_solution(18370941719893394308)
XLA Ops:
  0.0 186.5 %shard_map.46 = f32[256,512]{1,0:T(8,128)} custom-call(f32[4032,512]{1,0:T(8,128)} %tail_hbm.1, f32[504,1024]{1,0:T(8,128)} %panel_hbm.1, f32[32,1024]{1,0:T(8,128)} %block_hbm.1, f32[256,512]{1,0:T(8,128)} %rhs_hbm.1), custom_call_target="tpu_custom_call" | custom-call | tf_op jit(solution)/shard_map/pallas_call | solution.py:269
  186.6 1.9 copy.6
